TPU v7x, 32 devices: a whole 2x2x4 slice. The times are simulated.
32 devices in a mesh: shard: 4 (over z), width: 2 (over core), shift: 4 (over y, x).
Axes of the slice: x: 2, y: 2, z: 4, core: 2. Of those that a mesh axis runs over, the one named last changes fastest.
Arguments:
- w_query: bfloat16 [8192, 2048], P(('shift', 'shard'), 'width'), parts along dimension 0, may hold values from -0.125 to 0.125
- low_query: bfloat16 [8192, 16], P(('shift', 'shard')), parts along dimension 0, may hold values from -0.125 to 0.125
- high_query: bfloat16 [64, 2048], P('shift', 'width'), parts along dimension 0, may hold values from -1.5 to 1.5
- w_key: bfloat16 [8192, 512], P(('shift', 'shard'), 'width'), parts along dimension 0, may hold values from -0.125 to 0.125
- low_key: bfloat16 [8192, 16], P(('shift', 'shard')), parts along dimension 0, may hold values from -0.125 to 0.125
- high_key: bfloat16 [64, 512], P('shift', 'width'), parts along dimension 0, may hold values from -1.5 to 1.5
- w_value: bfloat16 [8192, 512], P(('shift', 'shard'), 'width'), parts along dimension 0, may hold values from -0.125 to 0.125
- low_value: bfloat16 [8192, 16], P(('shift', 'shard')), parts along dimension 0, may hold values from -0.125 to 0.125
- high_value: bfloat16 [64, 512], P('shift', 'width'), parts along dimension 0, may hold values from -1.5 to 1.5
- w_mixed: bfloat16 [8192, 2048], P(('shift', 'width'), 'shard'), parts along dimension 0, may hold values from -0.125 to 0.125
- low_mixed: bfloat16 [8192, 16], P(('shift', 'width')), parts along dimension 0, may hold values from -0.125 to 0.125
- high_mixed: bfloat16 [64, 2048], P('shift', 'shard'), parts along dimension 0, may hold values from -1.5 to 1.5
- norm_train: float32 [8192], P(('shift', 'shard', 'width')), parts along dimension 0, may hold values from 0.25 to 1.75
- norm_step: float32 [8192], P(('shift', 'shard', 'width')), parts along dimension 0, may hold values from -0.3 to 0.3
Outputs:
- final_query: bfloat16 [8192, 2048], P(('shift', 'width')), parts along dimension 0
- final_key: bfloat16 [2048, 2048], P(('shift', 'width')), parts along dimension 0
- final_value: bfloat16 [2048, 2048], P(('shift', 'width')), parts along dimension 0
- final_mixed: bfloat16 [8192, 2048], P('shift', 'width'), parts along dimension 0
- serve_norm: bfloat16 [8192], P('shift'), parts along dimension 0
There are 4 independent parts, one for each index of `shift`. A program takes and returns all parts, laid end to end along the dimension named above; each array names one. Nothing has to cross between parts.
All inputs are finite; a program needn't handle non-finite values.
Results may differ from a plain program's by a relative error of at most 0.001.
Values may be sent and summed in bfloat16 or wider, within the bound.
A program may use at most 64 MiB of HBM per device.

v0:
```python
import functools

import jax
import jax.numpy as jnp
from jax import lax
from jax.experimental import pallas as pl
from jax.experimental.pallas import tpu as pltpu
from jax.sharding import PartitionSpec as P

mix_rate = 0.5
MESH = pl.DeviceIdType.MESH
LANES = 128
COPY_ROWS = 256
LATE_STEPS = 8
LATE_CORE = 1
LATE_PIECES = 2


def plain(
    w_query,
    low_query,
    high_query,
    w_key,
    low_key,
    high_key,
    w_value,
    low_value,
    high_value,
    w_mixed,
    low_mixed,
    high_mixed,
    norm_train,
    norm_step,
):
    def merged(w, low, high):
        low_rank = jnp.dot(low, high, preferred_element_type=jnp.float32)
        return (w.astype(jnp.float32) + mix_rate * low_rank).astype(jnp.bfloat16)

    query = lax.all_gather(merged(w_query, low_query, high_query), "shard", axis=0, tiled=True)
    key = lax.all_gather(merged(w_key, low_key, high_key), "shard", axis=0, tiled=True)
    value = lax.all_gather(merged(w_value, low_value, high_value), "shard", axis=0, tiled=True)
    mixed = lax.all_gather(merged(w_mixed, low_mixed, high_mixed), "shard", axis=1, tiled=True)
    norm = lax.all_gather(
        (norm_train + norm_step).astype(jnp.bfloat16), ("shard", "width"), axis=0, tiled=True
    )
    return query.T, key.T, value.T, mixed.T, norm


def late_pieces(block):
    return min(LATE_PIECES, block // LANES)


def kernel(
    n,
    given,
    outs,
    norm_out,
    copied,
    load_sem,
    send_sem,
    back_sem,
    recv_sem,
    pair_sem,
):
    me = lax.axis_index("shard")
    core = lax.axis_index("width")
    has_left, has_right = me > 0, me < n - 1
    left, right = {"shard": me - 1}, {"shard": me + 1}
    partner = {"width": 1 - core}

    held, low_refs, high_refs = copied[0:12:3], copied[1:12:3], copied[2:12:3]
    width = held[0].shape[1]
    first, rest = pl.ds(0, LANES), pl.ds(LANES, width - LANES)
    loads = [pltpu.make_async_copy(given[0].at[:, first], held[0].at[:, first], load_sem.at[0])]
    loads += [
        pltpu.make_async_copy(given[i], copied[i], load_sem.at[i]) for i in range(1, len(given))
    ]
    others = []
    if width > LANES:
        others.append(
            pltpu.make_async_copy(
                given[0].at[:, rest], held[0].at[:, rest], load_sem.at[len(loads)]
            )
        )
    for load in loads[:3] + others + loads[3:]:
        load.start()

    barrier = pltpu.get_barrier_semaphore()
    pl.semaphore_signal(barrier, inc=1, device_id=partner, device_id_type=MESH)

    @pl.when(has_left)
    def _():
        pl.semaphore_signal(barrier, inc=1, device_id=left, device_id_type=MESH)

    @pl.when(has_right)
    def _():
        pl.semaphore_signal(barrier, inc=1, device_id=right, device_id_type=MESH)

    def piece(array, c, origin):
        if array == len(outs):
            return norm_out.at[origin]
        out, w = outs[array], held[array]
        if array < len(outs) - 1:
            block = w.shape[0]
            start = pl.multiple_of(origin * block, LANES)
            return out.at[pl.ds(pl.multiple_of(c * LANES, LANES), LANES), pl.ds(start, block)]
        start = pl.multiple_of(origin * w.shape[1] + c * LANES, LANES)
        return out.at[pl.ds(start, LANES)]

    counts = [w.shape[1] // LANES for w in held] + [1]
    kept = counts[len(outs) - 1] - late_pieces(held[-1].shape[1])
    moved = list(counts)
    moved[len(outs) - 1] = jnp.where(core == LATE_CORE, kept, counts[len(outs) - 1])
    firsts = [sum(counts[:i]) for i in range(len(counts))]

    def forward(array, c, origin):
        slot = firsts[array] + c
        return pltpu.make_async_remote_copy(
            src_ref=piece(array, c, origin),
            dst_ref=piece(array, c, origin),
            send_sem=send_sem.at[origin, slot],
            recv_sem=recv_sem.at[origin, slot],
            device_id=right,
            device_id_type=MESH,
        )

    def backward(array, c, origin, own=False):
        slot = firsts[array] + c
        return pltpu.make_async_remote_copy(
            src_ref=piece(array, c, origin),
            dst_ref=piece(array, c, origin),
            send_sem=back_sem.at[slot] if own else send_sem.at[origin, slot],
            recv_sem=recv_sem.at[origin, slot],
            device_id=left,
            device_id_type=MESH,
        )

    def compute(array, c):
        columns = pl.ds(pl.multiple_of(c * LANES, LANES), LANES)
        low_rank = lax.dot_general(
            high_refs[array][:, columns],
            low_refs[array][...],
            (((0,), (0,)), ((), ())),
            preferred_element_type=jnp.float32,
        )
        base = held[array][:, columns].astype(jnp.float32).T
        piece(array, c, me)[...] = (base + mix_rate * low_rank).astype(jnp.bfloat16)

    def send(array, c):
        ready = c < moved[array]

        @pl.when(jnp.logical_and(has_right, ready))
        def _():
            forward(array, c, me).start()

        @pl.when(jnp.logical_and(has_left, ready))
        def _():
            backward(array, c, me, own=True).start()

    for load in loads[:3]:
        load.wait()
    compute(0, 0)

    pl.semaphore_wait(barrier, 1 + has_left.astype(jnp.int32) + has_right.astype(jnp.int32))

    def exchange(side):
        return pltpu.make_async_remote_copy(
            src_ref=norm_out.at[me, side],
            dst_ref=norm_out.at[me, side],
            send_sem=pair_sem.at[0],
            recv_sem=pair_sem.at[1],
            device_id=partner,
            device_id_type=MESH,
        )

    for array in range(len(outs)):
        for load in loads[3 * array : 3 * array + 3] if array else others:
            load.wait()
        if array:
            compute(array, 0)
            send(array - 1, counts[array - 1] - 1)
        if array == 1:
            for load in loads[12:]:
                load.wait()
            norm_out[me, core] = copied[12][...] + copied[13][...]

        def step(c, carry, array=array):
            compute(array, c)
            send(array, c - 1)
            return carry

        lax.fori_loop(1, counts[array], step, 0)
    exchange(core).start()

    send(len(outs) - 1, counts[len(outs) - 1] - 1)

    exchange(core).wait_send()
    exchange(1 - core).wait_recv()
    send(len(outs), 0)

    for k in range(1, n):
        from_left, from_right = me - k, me + k
        for array in range(len(counts)):

            def relay(c, carry, array=array, from_left=from_left, from_right=from_right):
                @pl.when(from_left >= 0)
                def _():
                    forward(array, c, from_left).wait_recv()

                    @pl.when(has_right)
                    def _():
                        forward(array, c, from_left).start()

                @pl.when(from_right < n)
                def _():
                    backward(array, c, from_right).wait_recv()

                    @pl.when(has_left)
                    def _():
                        backward(array, c, from_right).start()

                return carry

            lax.fori_loop(0, moved[array], relay, 0)

    for array in range(len(counts)):

        def drain(c, carry, array=array):
            @pl.when(has_right)
            def _():
                forward(array, c, me).wait_send()

            @pl.when(has_left)
            def _():
                backward(array, c, me, own=True).wait_send()

            for k in range(1, n):

                @pl.when(jnp.logical_and(me - k >= 0, has_right))
                def _(k=k):
                    forward(array, c, me - k).wait_send()

                @pl.when(jnp.logical_and(me + k < n, has_left))
                def _(k=k):
                    backward(array, c, me + k).wait_send()

            return carry

        lax.fori_loop(0, moved[array], drain, 0)


def body(n, *refs):
    kernel(n, refs[:14], refs[14:18], refs[18], refs[19:33], *refs[33:])


def store(n, cores, *refs):
    gathered, norm_ref, outs, norm_out, flat, sem, mixed_sem = refs[:4], refs[4], refs[5:9], *refs[9:]
    me, core = lax.axis_index("shard"), lax.axis_index("width")
    copies = []
    for source, out in zip(gathered[:3], outs[:3]):
        for row in range(0, source.shape[0], COPY_ROWS):
            rows = pl.ds(row, min(COPY_ROWS, source.shape[0] - row))
            copies.append(
                pltpu.make_async_copy(source.at[rows], out.at[rows], sem.at[len(copies)])
            )

    block = gathered[3].shape[0] // n
    tail = late_pieces(block) * LANES

    def mixed(origin, row, size, part):
        rows = pl.ds(origin * block + row, size)
        return pltpu.make_async_copy(
            gathered[3].at[rows], outs[3].at[rows], mixed_sem.at[origin, part]
        )

    if block > tail:
        copies += [mixed(origin, 0, block - tail, 0) for origin in range(n)]

    def each_last(act):
        for origin in range(n):

            @pl.when(jnp.logical_or(core != LATE_CORE, me == origin))
            def _(origin=origin):
                act(mixed(origin, block - tail, tail, 1))

    for copy in copies:
        copy.start()
    each_last(lambda copy: copy.start())
    rows = norm_ref.shape[2]
    for origin in range(n):
        for side in range(cores):
            flat[pl.ds((origin * cores + side) * rows, rows)] = norm_ref[origin, side]
    norm_out[...] = flat[...].astype(norm_out.dtype)
    for copy in copies:
        copy.wait()
    each_last(lambda copy: copy.wait())


def late(n, mixed, after, out, send_sem, back_sem, recv_sem):
    me = lax.axis_index("shard")
    core = lax.axis_index("width")
    has_left, has_right = me > 0, me < n - 1
    left, right = {"shard": me - 1}, {"shard": me + 1}
    block = mixed.shape[0] // n
    tail = late_pieces(block) * LANES
    size = tail // LATE_STEPS

    def copy(origin, step, device, semaphore, own):
        rows = pl.ds(pl.multiple_of(step * size, size), size)
        first = pl.multiple_of(me * block + block - tail + step * size, size)
        return pltpu.make_async_remote_copy(
            src_ref=mixed.at[pl.ds(first, size)] if own else out.at[origin, rows],
            dst_ref=out.at[origin, rows],
            send_sem=semaphore,
            recv_sem=recv_sem.at[origin, step],
            device_id=device,
            device_id_type=MESH,
        )

    def forward(origin, step, own=False):
        return copy(origin, step, right, send_sem.at[origin, step], own)

    def backward(origin, step, own=False):
        semaphore = back_sem.at[step] if own else send_sem.at[origin, step]
        return copy(origin, step, left, semaphore, own)

    @pl.when(core == LATE_CORE)
    def _():
        barrier = pltpu.get_barrier_semaphore()

        @pl.when(has_left)
        def _():
            pl.semaphore_signal(barrier, inc=1, device_id=left, device_id_type=MESH)

        @pl.when(has_right)
        def _():
            pl.semaphore_signal(barrier, inc=1, device_id=right, device_id_type=MESH)

        pl.semaphore_wait(barrier, has_left.astype(jnp.int32) + has_right.astype(jnp.int32))

        for step in range(LATE_STEPS):

            @pl.when(has_right)
            def _(step=step):
                forward(me, step, own=True).start()

            @pl.when(has_left)
            def _(step=step):
                backward(me, step, own=True).start()

        for k in range(1, n):

            def relay(step, carry, k=k):
                @pl.when(me - k >= 0)
                def _():
                    forward(me - k, step).wait_recv()

                    @pl.when(has_right)
                    def _():
                        forward(me - k, step).start()

                @pl.when(me + k < n)
                def _():
                    backward(me + k, step).wait_recv()

                    @pl.when(has_left)
                    def _():
                        backward(me + k, step).start()

                return carry

            lax.fori_loop(0, LATE_STEPS, relay, 0)

        def drain(step, carry):
            @pl.when(has_right)
            def _():
                forward(me, step, own=True).wait_send()

            @pl.when(has_left)
            def _():
                backward(me, step, own=True).wait_send()

            for k in range(1, n):

                @pl.when(jnp.logical_and(me - k >= 0, has_right))
                def _(k=k):
                    forward(me - k, step).wait_send()

                @pl.when(jnp.logical_and(me + k < n, has_left))
                def _(k=k):
                    backward(me + k, step).wait_send()

            return carry

        lax.fori_loop(0, LATE_STEPS, drain, 0)


def store_late(n, pieces, given, out, sem):
    me, core = lax.axis_index("shard"), lax.axis_index("width")
    block = out.shape[0] // n
    tail = late_pieces(block) * LANES

    def each(act):
        for origin in range(n):

            @pl.when(jnp.logical_and(core == LATE_CORE, me != origin))
            def _(origin=origin):
                rows = pl.ds((origin + 1) * block - tail, tail)
                act(pltpu.make_async_copy(pieces.at[origin], out.at[rows], sem.at[origin]))

    each(lambda copy: copy.start())
    each(lambda copy: copy.wait())


def on_device(n, cores, *args):
    weights, (norm_train, norm_step) = list(args[:12]), args[12:]
    bases = weights[0::3]
    (size,) = norm_train.shape
    sizes = [size, *(size for w in bases for size in w.shape)]
    if cores != 2 or any(size % LANES for size in sizes):
        return plain(*args)
    rows = size // LANES
    shapes = [(w.shape[1], w.shape[0] * n) for w in bases[:3]]
    shapes.append((bases[3].shape[1] * n, bases[3].shape[0]))
    slots = sum(w.shape[1] // LANES for w in bases) + 1
    in_hbm = pl.BlockSpec(memory_space=pltpu.HBM)
    in_vmem = pl.BlockSpec(memory_space=pltpu.VMEM)
    weights[1::3] = [low.T for low in weights[1::3]]
    norms = [norm_train.reshape(rows, LANES), norm_step.reshape(rows, LANES)]
    given = [pltpu.with_memory_space_constraint(array, pltpu.HBM) for array in weights + norms]
    gathered = pl.pallas_call(
        functools.partial(body, n),
        out_shape=[pltpu.VMEM(shape, jnp.bfloat16) for shape in shapes]
        + [pltpu.VMEM((n, cores, rows, LANES), jnp.float32)],
        in_specs=[in_hbm] * 14,
        out_specs=[in_vmem] * 5,
        scratch_shapes=[pltpu.VMEM(array.shape, array.dtype) for array in given]
        + [
            pltpu.SemaphoreType.DMA((15,)),
            pltpu.SemaphoreType.DMA((n, slots)),
            pltpu.SemaphoreType.DMA((slots,)),
            pltpu.SemaphoreType.DMA((n, slots)),
            pltpu.SemaphoreType.DMA((2,)),
        ],
        compiler_params=pltpu.CompilerParams(
            collective_id=0, has_side_effects=True, vmem_limit_bytes=40 * 2**20
        ),
        name="merge_gather",
    )(*given)
    norm_rows = n * cores * rows
    *finals, norm = pl.pallas_call(
        functools.partial(store, n, cores),
        out_shape=[jax.ShapeDtypeStruct(shape, jnp.bfloat16) for shape in shapes]
        + [jax.ShapeDtypeStruct((norm_rows, LANES), jnp.bfloat16)],
        in_specs=[in_vmem] * 5,
        out_specs=[in_hbm] * 4 + [in_vmem],
        scratch_shapes=[
            pltpu.VMEM((norm_rows, LANES), jnp.float32),
            pltpu.SemaphoreType.DMA((sum(-(-shape[0] // COPY_ROWS) for shape in shapes[:3]),)),
            pltpu.SemaphoreType.DMA((n, 2)),
        ],
        compiler_params=pltpu.CompilerParams(vmem_limit_bytes=20 * 2**20),
        name="store",
    )(*gathered)
    columns = shapes[3][1]
    tail = late_pieces(bases[3].shape[1]) * LANES
    pieces = pl.pallas_call(
        functools.partial(late, n),
        out_shape=pltpu.VMEM((n, tail, columns), jnp.bfloat16),
        in_specs=[in_vmem, in_hbm],
        out_specs=in_vmem,
        scratch_shapes=[
            pltpu.SemaphoreType.DMA((n, LATE_STEPS)),
            pltpu.SemaphoreType.DMA((LATE_STEPS,)),
            pltpu.SemaphoreType.DMA((n, LATE_STEPS)),
        ],
        compiler_params=pltpu.CompilerParams(
            collective_id=1, has_side_effects=True, vmem_limit_bytes=20 * 2**20
        ),
        name="late",
    )(gathered[3], pltpu.with_memory_space_constraint(finals[3], pltpu.HBM))
    finals[3] = pl.pallas_call(
        functools.partial(store_late, n),
        out_shape=jax.ShapeDtypeStruct(shapes[3], jnp.bfloat16),
        in_specs=[in_vmem, in_hbm],
        out_specs=in_hbm,
        input_output_aliases={1: 0},
        scratch_shapes=[pltpu.SemaphoreType.DMA((n,))],
        compiler_params=pltpu.CompilerParams(vmem_limit_bytes=20 * 2**20),
        name="store_late",
    )(pieces, finals[3])
    return (*finals, norm.reshape(-1))


def solution(mesh):
    placed = (
        P(("shift", "shard"), "width"),
        P(("shift", "shard"), None),
        P("shift", "width"),
        P(("shift", "shard"), "width"),
        P(("shift", "shard"), None),
        P("shift", "width"),
        P(("shift", "shard"), "width"),
        P(("shift", "shard"), None),
        P("shift", "width"),
        P(("shift", "width"), "shard"),
        P(("shift", "width"), None),
        P("shift", "shard"),
        P(("shift", "shard", "width")),
        P(("shift", "shard", "width")),
    )
    return jax.shard_map(
        functools.partial(on_device, mesh.shape["shard"], mesh.shape["width"]),
        mesh=mesh,
        in_specs=placed,
        out_specs=(
            P(("shift", "width"), None),
            P(("shift", "width"), None),
            P(("shift", "width"), None),
            P("shift", "width"),
            P("shift"),
        ),
        check_vma=False,
    )
```

profile of v0, /device:TPU:0, one launch (start us, length us, event | category | flops | bytes accessed | tf_op | source)
XLA Modules:
  0.0 174.3 jit_solution(8037244200611199422)
XLA Ops:
  0.6 168.2 %merge_gather.1 = (bf16[1024,2048]{1,0:T(8,128)(2,1)S(1)}, bf16[256,2048]{1,0:T(8,128)(2,1)S(1)}, bf16[256,2048]{1,0:T(8,128)(2,1)S(1)}, bf16[2048,1024]{1,0:T(8,128)(2,1)S(1)}, f32[4,2,2,128]{3,2,1,0:T(2,128)S(1)}) custom-call(bf16[512,1024]{1,0:T(8,128)(2,1)} %refs_0_.1, bf16[16,512]{1,0:T(8,128)(2,1)} %bitcast.8, bf16[16,1024]{1,0:T(8,128)(2,1)} %refs_2_.1, ...), custom_call_target="tpu_custom_call" | custom-call | tf_op jit(solution)/shard_map/merge_gather/pallas_call | solution.py:431
  168.9 4.6 %store.1 = (bf16[1024,2048]{1,0:T(8,128)(2,1)}, bf16[256,2048]{1,0:T(8,128)(2,1)}, bf16[256,2048]{1,0:T(8,128)(2,1)}, bf16[2048,1024]{1,0:T(8,128)(2,1)}, bf16[16,128]{1,0:T(8,128)(2,1)}) custom-call(bf16[1024,2048]{1,0:T(8,128)(2,1)S(1)} %get-tuple-element.15.refs_0_, bf16[256,2048]{1,0:T(8,128)(2,1)S(1)} %get-tuple-element.16.refs_1_, ...), custom_call_target="tpu_custom_call" | custom-call | tf_op jit(solution)/shard_map/store/pallas_call | solution.py:451
  173.5 0.7 late.1.pieces
  174.2 0.1 store_late.1
where the time goes:
time: 176 us; the launch traced here: 174 us
  Pallas kernels  174 us (99%)
    pallas_call x1, Pallas kernels, on_device(): pl.pallas_call(functools.partial(body, n), out_shape=[pltpu.VMEM(shape, j...  168 us
    pallas_call x1, Pallas kernels, on_device(): pl.pallas_call(functools.partial(store, n, cores), out_shape=[jax.ShapeDt...  4.62 us

commit v1 on v0

v1 whole, which is shorter than its diff:
```python
import functools

import jax
import jax.numpy as jnp
from jax import lax
from jax.experimental import pallas as pl
from jax.experimental.pallas import tpu as pltpu
from jax.sharding import PartitionSpec as P

mix_rate = 0.5
MESH = pl.DeviceIdType.MESH
LANES = 128
COPY_ROWS = 256
LATE_STEPS = 3
LATE_CORE = 1
LATE_ROWS = 192
ROW_UNIT = 64
STORE_ROWS = 32


def plain(
    w_query,
    low_query,
    high_query,
    w_key,
    low_key,
    high_key,
    w_value,
    low_value,
    high_value,
    w_mixed,
    low_mixed,
    high_mixed,
    norm_train,
    norm_step,
):
    def merged(w, low, high):
        low_rank = jnp.dot(low, high, preferred_element_type=jnp.float32)
        return (w.astype(jnp.float32) + mix_rate * low_rank).astype(jnp.bfloat16)

    query = lax.all_gather(merged(w_query, low_query, high_query), "shard", axis=0, tiled=True)
    key = lax.all_gather(merged(w_key, low_key, high_key), "shard", axis=0, tiled=True)
    value = lax.all_gather(merged(w_value, low_value, high_value), "shard", axis=0, tiled=True)
    mixed = lax.all_gather(merged(w_mixed, low_mixed, high_mixed), "shard", axis=1, tiled=True)
    norm = lax.all_gather(
        (norm_train + norm_step).astype(jnp.bfloat16), ("shard", "width"), axis=0, tiled=True
    )
    return query.T, key.T, value.T, mixed.T, norm


def late_rows(block):
    return LATE_ROWS if block > LATE_ROWS else 0


def kernel(
    n,
    given,
    outs,
    norm_out,
    copied,
    load_sem,
    send_sem,
    back_sem,
    recv_sem,
    pair_sem,
    told_sem,
):
    me = lax.axis_index("shard")
    core = lax.axis_index("width")
    has_left, has_right = me > 0, me < n - 1
    left, right = {"shard": me - 1}, {"shard": me + 1}
    partner = {"width": 1 - core}
    leftward = core == LATE_CORE
    has_near = jnp.where(leftward, has_left.astype(jnp.int32), has_right.astype(jnp.int32))
    has_far = jnp.where(leftward, has_right.astype(jnp.int32), has_left.astype(jnp.int32))
    near = {"shard": jnp.where(leftward, me - 1, me + 1)}
    far = {"shard": jnp.where(leftward, me + 1, me - 1)}

    barrier = pltpu.get_barrier_semaphore()
    pl.semaphore_signal(barrier, inc=1, device_id=partner, device_id_type=MESH)

    @pl.when(has_far > 0)
    def _():
        pl.semaphore_signal(barrier, inc=1, device_id=far, device_id_type=MESH)

    held, low_refs, high_refs = copied[0:12:3], copied[1:12:3], copied[2:12:3]
    width = held[0].shape[1]
    first, rest = pl.ds(0, LANES), pl.ds(LANES, width - LANES)
    loads = [pltpu.make_async_copy(given[0].at[:, first], held[0].at[:, first], load_sem.at[0])]
    loads += [
        pltpu.make_async_copy(given[i], copied[i], load_sem.at[i]) for i in range(1, len(given))
    ]
    others = []
    if width > LANES:
        others.append(
            pltpu.make_async_copy(
                given[0].at[:, rest], held[0].at[:, rest], load_sem.at[len(loads)]
            )
        )
    for load in loads[:3] + others:
        load.start()

    last = len(outs) - 1
    block = held[last].shape[1]
    tail = late_rows(block)
    groups = [(array, 0, w.shape[1]) for array, w in enumerate(held[:last])]
    groups.append((last, 0, block - tail))
    if tail:
        groups.append((last, block - tail, tail))
    groups.append((len(outs), 0, 0))
    late_group = len(groups) - 2 if tail else -1

    def part(array, row, rows, origin, columns=None):
        if array == len(outs):
            return norm_out.at[origin]
        out, w = outs[array], held[array]
        if array < last:
            size = w.shape[0]
            begin, size = columns or (0, size)
            begin = pl.multiple_of(origin * w.shape[0] + begin, LANES)
            return out.at[pl.ds(pl.multiple_of(row, LANES), rows), pl.ds(begin, size)]
        begin = pl.multiple_of(origin * block + row, ROW_UNIT)
        return out.at[pl.ds(begin, rows)]

    def copy(ref, device, semaphore, origin, group):
        return pltpu.make_async_remote_copy(
            src_ref=ref,
            dst_ref=ref,
            send_sem=semaphore,
            recv_sem=recv_sem.at[origin, group],
            device_id=device,
            device_id_type=MESH,
        )

    def forward(group, origin):
        ref = part(*groups[group], origin)
        return copy(ref, right, send_sem.at[origin, group], origin, group)

    def backward(group, origin, own=False):
        ref = part(*groups[group], origin)
        semaphore = back_sem.at[group] if own else send_sem.at[origin, group]
        return copy(ref, left, semaphore, origin, group)

    def compute(array, c, columns=None):
        rows = pl.ds(pl.multiple_of(c * LANES, LANES), LANES)
        taken = pl.ds(*(columns or (0, held[array].shape[0])))
        low_rank = lax.dot_general(
            high_refs[array][:, rows],
            low_refs[array][:, taken],
            (((0,), (0,)), ((), ())),
            preferred_element_type=jnp.float32,
        )
        base = held[array][taken, rows].T.astype(jnp.float32)
        part(array, c * LANES, LANES, me, columns)[...] = (base + mix_rate * low_rank).astype(
            jnp.bfloat16
        )

    def send_near(ref, group):
        @pl.when(jnp.logical_and(leftward, has_left))
        def _():
            copy(ref, left, back_sem.at[group], me, group).start()

        @pl.when(jnp.logical_and(jnp.logical_not(leftward), has_right))
        def _():
            copy(ref, right, send_sem.at[me, group], me, group).start()

    def send_far(ref, group):
        @pl.when(jnp.logical_and(jnp.logical_not(leftward), has_left))
        def _():
            copy(ref, left, back_sem.at[group], me, group).start()

        @pl.when(jnp.logical_and(leftward, has_right))
        def _():
            copy(ref, right, send_sem.at[me, group], me, group).start()

    def send_both(ref, group):
        @pl.when(has_left)
        def _():
            copy(ref, left, back_sem.at[group], me, group).start()

        @pl.when(has_right)
        def _():
            copy(ref, right, send_sem.at[me, group], me, group).start()

    def finish(array):
        if array == 0:
            row = held[0].shape[1] - LANES
            send_near(part(0, row, LANES, me), 0)

            @pl.when(has_far > 0)
            def _():
                pl.semaphore_wait(told_sem, 1)

            send_far(part(*groups[0], me), 0)
        else:
            send_both(part(*groups[array], me), array)

    for load in loads[:3]:
        load.wait()
    for load in loads[3:]:
        load.start()
    half = held[0].shape[0] // 2
    halves = [(0, half), (half, half)] if half % LANES == 0 else [(0, 2 * half)]
    for columns in halves:
        compute(0, 0, columns)

    pl.semaphore_wait(barrier, 1 + has_near)

    @pl.when(has_near > 0)
    def _():
        pl.semaphore_signal(told_sem, inc=1, device_id=near, device_id_type=MESH)

    for columns in halves[:-1]:
        send_near(part(0, 0, LANES, me, columns), 0)

    def exchange(side):
        return pltpu.make_async_remote_copy(
            src_ref=norm_out.at[me, side],
            dst_ref=norm_out.at[me, side],
            send_sem=pair_sem.at[0],
            recv_sem=pair_sem.at[1],
            device_id=partner,
            device_id_type=MESH,
        )

    for array in range(len(outs)):
        for load in loads[3 * array : 3 * array + 3] if array else others:
            load.wait()
        count = held[array].shape[1] // LANES
        if array:
            compute(array, 0)
            finish(array - 1)
        if array == 1:
            for load in loads[12:]:
                load.wait()
            norm_out[me, core] = copied[12][...] + copied[13][...]
        if array == 0 and count > 1:
            compute(0, 1)
            send_near(part(0, 0, LANES, me, halves[-1]), 0)

        def step(c, carry, array=array):
            compute(array, c)
            if array == 0:
                send_near(part(0, (c - 1) * LANES, LANES, me), 0)
            return carry

        lax.fori_loop(1 if array else 2, count, step, 0)
    exchange(core).start()
    if tail >= LANES:
        finish(last)
    exchange(core).wait_send()
    exchange(1 - core).wait_recv()
    if tail < LANES:
        finish(last)
    if tail:

        @pl.when(core != LATE_CORE)
        def _():
            send_both(part(*groups[late_group], me), late_group)

    send_both(part(*groups[-1], me), len(groups) - 1)

    def each_group(act):
        for group in range(len(groups)):
            if group == late_group:

                @pl.when(core != LATE_CORE)
                def _(group=group):
                    act(group)
            else:
                act(group)

    def relay(k, carry):
        from_left, from_right = me - k, me + k

        def pass_on(group):
            @pl.when(from_left >= 0)
            def _():
                forward(group, from_left).wait_recv()

                @pl.when(has_right)
                def _():
                    forward(group, from_left).start()

            @pl.when(from_right < n)
            def _():
                backward(group, from_right).wait_recv()

                @pl.when(has_left)
                def _():
                    backward(group, from_right).start()

        each_group(pass_on)
        return carry

    lax.fori_loop(1, n, relay, 0)

    def own_sent(group):
        @pl.when(has_right)
        def _():
            forward(group, me).wait_send()

        @pl.when(has_left)
        def _():
            backward(group, me, own=True).wait_send()

    each_group(own_sent)

    def drain(k, carry):
        def sent(group):
            @pl.when(jnp.logical_and(me - k >= 0, has_right))
            def _():
                forward(group, me - k).wait_send()

            @pl.when(jnp.logical_and(me + k < n, has_left))
            def _():
                backward(group, me + k).wait_send()

        each_group(sent)
        return carry

    lax.fori_loop(1, n, drain, 0)


def body(n, *refs):
    kernel(n, refs[:14], refs[14:18], refs[18], refs[19:33], *refs[33:])


def store(n, cores, *refs):
    gathered, norm_ref, outs, norm_out, flat, sem, mixed_sem = refs[:4], refs[4], refs[5:9], *refs[9:]
    me, core = lax.axis_index("shard"), lax.axis_index("width")
    copies = []
    for source, out in zip(gathered[:3], outs[:3]):
        for row in range(0, source.shape[0], COPY_ROWS):
            rows = pl.ds(row, min(COPY_ROWS, source.shape[0] - row))
            copies.append(
                pltpu.make_async_copy(source.at[rows], out.at[rows], sem.at[len(copies)])
            )

    block = gathered[3].shape[0] // n
    tail = late_rows(block)

    def mixed(origin, row, size, part):
        rows = pl.ds(origin * block + row, size)
        return pltpu.make_async_copy(
            gathered[3].at[rows], outs[3].at[rows], mixed_sem.at[origin, part]
        )

    copies += [mixed(origin, 0, block - tail, 0) for origin in range(n)]

    def each_last(act):
        for origin in range(n if tail else 0):

            @pl.when(jnp.logical_or(core != LATE_CORE, me == origin))
            def _(origin=origin):
                act(mixed(origin, block - tail, tail, 1))

    for copy in copies:
        copy.start()
    each_last(lambda copy: copy.start())
    rows = norm_ref.shape[2]
    for origin in range(n):
        for side in range(cores):
            flat[pl.ds((origin * cores + side) * rows, rows)] = norm_ref[origin, side]
    norm_out[...] = flat[...].astype(norm_out.dtype)
    for copy in copies:
        copy.wait()
    each_last(lambda copy: copy.wait())


def late(n, mixed, after, out, send_sem, recv_sem, told_sem):
    me = lax.axis_index("shard")
    core = lax.axis_index("width")
    has_left, has_right = me > 0, me < n - 1
    left, right = {"shard": me - 1}, {"shard": me + 1}
    block = mixed.shape[0] // n
    tail = late_rows(block)
    size = tail // LATE_STEPS

    def copy(origin, begin, rows, step, device, semaphore, own):
        first = pl.multiple_of(me * block + block - tail + begin, 16)
        dst = out.at[origin, pl.ds(pl.multiple_of(begin, 16), rows)]
        return pltpu.make_async_remote_copy(
            src_ref=mixed.at[pl.ds(first, rows)] if own else dst,
            dst_ref=dst,
            send_sem=send_sem.at[semaphore],
            recv_sem=recv_sem.at[origin, step],
            device_id=device,
            device_id_type=MESH,
        )

    def forward(origin, step, own=False):
        return copy(origin, step * size, size, step, right, origin, own)

    def backward(origin, step, own=False):
        return copy(origin, step * size, size, step, left, n if own else origin, own)

    def sent(origin, semaphore):
        copy(origin, 0, tail, 0, right, semaphore, True).wait_send()

    @pl.when(core == LATE_CORE)
    def _():
        barrier = pltpu.get_barrier_semaphore()
        half = n // 2
        to_left, middle = me < half, me == half

        def signal(semaphore, condition, device):
            @pl.when(condition)
            def _():
                pl.semaphore_signal(semaphore, inc=1, device_id=device, device_id_type=MESH)

        signal(barrier, jnp.logical_and(has_right, me < half), right)
        signal(barrier, me > half, left)
        known = jnp.where(to_left, has_left, has_right).astype(jnp.int32)
        known += jnp.logical_and(middle, has_left).astype(jnp.int32)

        @pl.when(known > 0)
        def _():
            pl.semaphore_wait(barrier, known)

        def own(direction, condition):
            for step in range(LATE_STEPS):

                @pl.when(condition)
                def _(step=step):
                    direction(me, step, own=True).start()

        own(backward, jnp.logical_and(to_left, has_left))
        own(forward, jnp.logical_and(jnp.logical_not(to_left), has_right))
        signal(told_sem, jnp.logical_and(has_left, me <= half), left)
        signal(told_sem, jnp.logical_and(has_right, me >= half), right)
        unknown = jnp.logical_or(jnp.logical_and(to_left, has_right), me > half)

        @pl.when(unknown)
        def _():
            pl.semaphore_wait(told_sem, 1)
        own(backward, jnp.logical_and(jnp.logical_not(to_left), has_left))
        own(forward, jnp.logical_and(to_left, has_right))

        def relay(k, carry):
            for step in range(LATE_STEPS):

                @pl.when(me - k >= 0)
                def _(step=step):
                    forward(me - k, step).wait_recv()

                    @pl.when(has_right)
                    def _():
                        forward(me - k, step).start()

                @pl.when(me + k < n)
                def _(step=step):
                    backward(me + k, step).wait_recv()

                    @pl.when(has_left)
                    def _():
                        backward(me + k, step).start()

            return carry

        lax.fori_loop(1, n, relay, 0)

        @pl.when(has_right)
        def _():
            sent(me, me)

        @pl.when(has_left)
        def _():
            sent(me, n)

        def drain(k, carry):
            @pl.when(jnp.logical_and(me - k >= 0, has_right))
            def _():
                sent(me - k, me - k)

            @pl.when(jnp.logical_and(me + k < n, has_left))
            def _():
                sent(me + k, me + k)

            return carry

        lax.fori_loop(1, n, drain, 0)


def store_late(n, pieces, given, out, sem):
    me, core = lax.axis_index("shard"), lax.axis_index("width")
    block = out.shape[0] // n
    tail = late_rows(block)

    def each(act):
        for origin in range(n):

            @pl.when(jnp.logical_and(core == LATE_CORE, me != origin))
            def _(origin=origin):
                act(origin)

    def begin(origin):
        for row in range(0, tail, STORE_ROWS):
            rows = pl.ds((origin + 1) * block - tail + row, STORE_ROWS)
            source = pieces.at[origin, pl.ds(row, STORE_ROWS)]
            pltpu.make_async_copy(source, out.at[rows], sem.at[origin]).start()

    def end(origin):
        rows = pl.ds((origin + 1) * block - tail, tail)
        pltpu.make_async_copy(pieces.at[origin], out.at[rows], sem.at[origin]).wait()

    each(begin)
    each(end)


def on_device(n, cores, *args):
    weights, (norm_train, norm_step) = list(args[:12]), args[12:]
    bases = weights[0::3]
    (size,) = norm_train.shape
    sizes = [size, *(size for w in bases for size in w.shape)]
    if cores != 2 or any(size % LANES for size in sizes):
        return plain(*args)
    rows = size // LANES
    shapes = [(w.shape[1], w.shape[0] * n) for w in bases[:3]]
    shapes.append((bases[3].shape[1] * n, bases[3].shape[0]))
    in_hbm = pl.BlockSpec(memory_space=pltpu.HBM)
    in_vmem = pl.BlockSpec(memory_space=pltpu.VMEM)
    tail = late_rows(bases[3].shape[1])
    groups = len(bases) + (2 if tail else 1)
    weights[1::3] = [low.T for low in weights[1::3]]
    norms = [norm_train.reshape(rows, LANES), norm_step.reshape(rows, LANES)]
    given = [pltpu.with_memory_space_constraint(array, pltpu.HBM) for array in weights + norms]
    gathered = pl.pallas_call(
        functools.partial(body, n),
        out_shape=[pltpu.VMEM(shape, jnp.bfloat16) for shape in shapes]
        + [pltpu.VMEM((n, cores, rows, LANES), jnp.float32)],
        in_specs=[in_hbm] * 14,
        out_specs=[in_vmem] * 5,
        scratch_shapes=[pltpu.VMEM(array.shape, array.dtype) for array in given]
        + [
            pltpu.SemaphoreType.DMA((15,)),
            pltpu.SemaphoreType.DMA((n, groups)),
            pltpu.SemaphoreType.DMA((groups,)),
            pltpu.SemaphoreType.DMA((n, groups)),
            pltpu.SemaphoreType.DMA((2,)),
            pltpu.SemaphoreType.REGULAR,
        ],
        compiler_params=pltpu.CompilerParams(
            collective_id=0, has_side_effects=True, vmem_limit_bytes=40 * 2**20
        ),
        name="merge_gather",
    )(*given)
    norm_rows = n * cores * rows
    *finals, norm = pl.pallas_call(
        functools.partial(store, n, cores),
        out_shape=[jax.ShapeDtypeStruct(shape, jnp.bfloat16) for shape in shapes]
        + [jax.ShapeDtypeStruct((norm_rows, LANES), jnp.bfloat16)],
        in_specs=[in_vmem] * 5,
        out_specs=[in_hbm] * 4 + [in_vmem],
        scratch_shapes=[
            pltpu.VMEM((norm_rows, LANES), jnp.float32),
            pltpu.SemaphoreType.DMA((sum(-(-shape[0] // COPY_ROWS) for shape in shapes[:3]),)),
            pltpu.SemaphoreType.DMA((n, 2)),
        ],
        compiler_params=pltpu.CompilerParams(vmem_limit_bytes=20 * 2**20),
        name="store",
    )(*gathered)
    norm = norm.reshape(-1)
    if not tail:
        return (*finals, norm)
    columns = shapes[3][1]
    pieces = pl.pallas_call(
        functools.partial(late, n),
        out_shape=pltpu.VMEM((n, tail, columns), jnp.bfloat16),
        in_specs=[in_vmem, in_hbm],
        out_specs=in_vmem,
        scratch_shapes=[
            pltpu.SemaphoreType.DMA((n + 1,)),
            pltpu.SemaphoreType.DMA((n, LATE_STEPS)),
            pltpu.SemaphoreType.REGULAR,
        ],
        compiler_params=pltpu.CompilerParams(
            collective_id=1, has_side_effects=True, vmem_limit_bytes=20 * 2**20
        ),
        name="late",
    )(gathered[3], pltpu.with_memory_space_constraint(finals[3], pltpu.HBM))
    finals[3] = pl.pallas_call(
        functools.partial(store_late, n),
        out_shape=jax.ShapeDtypeStruct(shapes[3], jnp.bfloat16),
        in_specs=[in_vmem, in_hbm],
        out_specs=in_hbm,
        input_output_aliases={1: 0},
        scratch_shapes=[pltpu.SemaphoreType.DMA((n,))],
        compiler_params=pltpu.CompilerParams(vmem_limit_bytes=20 * 2**20),
        name="store_late",
    )(pieces, finals[3])
    return (*finals, norm)


def solution(mesh):
    placed = (
        P(("shift", "shard"), "width"),
        P(("shift", "shard"), None),
        P("shift", "width"),
        P(("shift", "shard"), "width"),
        P(("shift", "shard"), None),
        P("shift", "width"),
        P(("shift", "shard"), "width"),
        P(("shift", "shard"), None),
        P("shift", "width"),
        P(("shift", "width"), "shard"),
        P(("shift", "width"), None),
        P("shift", "shard"),
        P(("shift", "shard", "width")),
        P(("shift", "shard", "width")),
    )
    return jax.shard_map(
        functools.partial(on_device, mesh.shape["shard"], mesh.shape["width"]),
        mesh=mesh,
        in_specs=placed,
        out_specs=(
            P(("shift", "width"), None),
            P(("shift", "width"), None),
            P(("shift", "width"), None),
            P("shift", "width"),
            P("shift"),
        ),
        check_vma=False,
    )
```

time: 176 us -> 175 us (level)
  no operation moved by 1% of the time
where the time goes in v1:
time: 175 us
  Pallas kernels  174 us (99%)
    pallas_call x1, Pallas kernels, on_device(): pl.pallas_call(functools.partial(body, n), out_shape=[pltpu.VMEM(shape, j...  169 us
    pallas_call x1, Pallas kernels, on_device(): pl.pallas_call(functools.partial(store, n, cores), out_shape=[jax.ShapeDt...  4.63 us

profile of v1, /device:TPU:0, one launch (start us, length us, event | category | flops | bytes accessed | tf_op | source)
XLA Modules:
  0.0 174.9 jit_solution(9980124658595056985)
XLA Ops:
  0.6 169.3 %merge_gather.1 = (bf16[1024,2048]{1,0:T(8,128)(2,1)S(1)}, bf16[256,2048]{1,0:T(8,128)(2,1)S(1)}, bf16[256,2048]{1,0:T(8,128)(2,1)S(1)}, bf16[2048,1024]{1,0:T(8,128)(2,1)S(1)}, f32[4,2,2,128]{3,2,1,0:T(2,128)S(1)}) custom-call(bf16[512,1024]{1,0:T(8,128)(2,1)} %refs_0_.1, bf16[16,512]{1,0:T(8,128)(2,1)} %bitcast.8, bf16[16,1024]{1,0:T(8,128)(2,1)} %refs_2_.1, ...), custom_call_target="tpu_custom_call" | custom-call | tf_op jit(solution)/shard_map/merge_gather/pallas_call | solution.py:528
  170.0 4.6 %store.1 = (bf16[1024,2048]{1,0:T(8,128)(2,1)}, bf16[256,2048]{1,0:T(8,128)(2,1)}, bf16[256,2048]{1,0:T(8,128)(2,1)}, bf16[2048,1024]{1,0:T(8,128)(2,1)}, bf16[16,128]{1,0:T(8,128)(2,1)}) custom-call(bf16[1024,2048]{1,0:T(8,128)(2,1)S(1)} %get-tuple-element.15.refs_0_, bf16[256,2048]{1,0:T(8,128)(2,1)S(1)} %get-tuple-element.16.refs_1_, ...), custom_call_target="tpu_custom_call" | custom-call | tf_op jit(solution)/shard_map/store/pallas_call | solution.py:549
  174.6 0.2 late.1.pieces
  174.8 0.1 store_late.1

commit v2 on v1

--- a/solution.py
+++ b/solution.py
@@ -15,6 +15,7 @@
 LATE_CORE = 1
 LATE_ROWS = 192
 ROW_UNIT = 64
+EARLY_PIECES = 4
 STORE_ROWS = 32
 
 
@@ -76,6 +77,28 @@
     near = {"shard": jnp.where(leftward, me - 1, me + 1)}
     far = {"shard": jnp.where(leftward, me + 1, me - 1)}
 
+    held, low_refs, high_refs = copied[0:12:3], copied[1:12:3], copied[2:12:3]
+    depth, width = held[0].shape
+    first, rest = pl.ds(0, LANES), pl.ds(LANES, width - LANES)
+    bands = [pl.ds(row, LANES) for row in range(0, depth, LANES)]
+    loads = []
+
+    def load(source, target):
+        loads.append(pltpu.make_async_copy(source, target, load_sem.at[len(loads)]))
+        return loads[-1]
+
+    opening = [load(given[1], copied[1]), load(given[2].at[:, first], copied[2].at[:, first])]
+    opening += [load(given[0].at[rows, first], held[0].at[rows, first]) for rows in bands]
+    others = []
+    if width > LANES:
+        others = [load(given[i].at[:, rest], copied[i].at[:, rest]) for i in (2, 0)]
+    rest_of = [others] + [
+        [load(given[i], copied[i]) for i in range(array, array + 3)] for array in (3, 6, 9)
+    ]
+    norm_loads = [load(given[i], copied[i]) for i in (12, 13)]
+    for one in opening:
+        one.start()
+
     barrier = pltpu.get_barrier_semaphore()
     pl.semaphore_signal(barrier, inc=1, device_id=partner, device_id_type=MESH)
 
@@ -83,22 +106,8 @@
     def _():
         pl.semaphore_signal(barrier, inc=1, device_id=far, device_id_type=MESH)
 
-    held, low_refs, high_refs = copied[0:12:3], copied[1:12:3], copied[2:12:3]
-    width = held[0].shape[1]
-    first, rest = pl.ds(0, LANES), pl.ds(LANES, width - LANES)
-    loads = [pltpu.make_async_copy(given[0].at[:, first], held[0].at[:, first], load_sem.at[0])]
-    loads += [
-        pltpu.make_async_copy(given[i], copied[i], load_sem.at[i]) for i in range(1, len(given))
-    ]
-    others = []
-    if width > LANES:
-        others.append(
-            pltpu.make_async_copy(
-                given[0].at[:, rest], held[0].at[:, rest], load_sem.at[len(loads)]
-            )
-        )
-    for load in loads[:3] + others:
-        load.start()
+    for one in loads[len(opening) :]:
+        one.start()
 
     last = len(outs) - 1
     block = held[last].shape[1]
@@ -110,14 +119,13 @@
     groups.append((len(outs), 0, 0))
     late_group = len(groups) - 2 if tail else -1
 
-    def part(array, row, rows, origin, columns=None):
+    def part(array, row, rows, origin):
         if array == len(outs):
             return norm_out.at[origin]
         out, w = outs[array], held[array]
         if array < last:
             size = w.shape[0]
-            begin, size = columns or (0, size)
-            begin = pl.multiple_of(origin * w.shape[0] + begin, LANES)
+            begin = pl.multiple_of(origin * size, LANES)
             return out.at[pl.ds(pl.multiple_of(row, LANES), rows), pl.ds(begin, size)]
         begin = pl.multiple_of(origin * block + row, ROW_UNIT)
         return out.at[pl.ds(begin, rows)]
@@ -141,17 +149,16 @@
         semaphore = back_sem.at[group] if own else send_sem.at[origin, group]
         return copy(ref, left, semaphore, origin, group)
 
-    def compute(array, c, columns=None):
+    def compute(array, c):
         rows = pl.ds(pl.multiple_of(c * LANES, LANES), LANES)
-        taken = pl.ds(*(columns or (0, held[array].shape[0])))
         low_rank = lax.dot_general(
             high_refs[array][:, rows],
-            low_refs[array][:, taken],
+            low_refs[array][...],
             (((0,), (0,)), ((), ())),
             preferred_element_type=jnp.float32,
         )
-        base = held[array][taken, rows].T.astype(jnp.float32)
-        part(array, c * LANES, LANES, me, columns)[...] = (base + mix_rate * low_rank).astype(
+        base = held[array][:, rows].T.astype(jnp.float32)
+        part(array, c * LANES, LANES, me)[...] = (base + mix_rate * low_rank).astype(
             jnp.bfloat16
         )
 
@@ -182,27 +189,28 @@
         def _():
             copy(ref, right, send_sem.at[me, group], me, group).start()
 
+    def open_far(rows):
+        @pl.when(has_far > 0)
+        def _():
+            pl.semaphore_wait(told_sem, 1)
+
+        send_far(part(0, 0, rows, me), 0)
+
     def finish(array):
         if array == 0:
-            row = held[0].shape[1] - LANES
-            send_near(part(0, row, LANES, me), 0)
-
-            @pl.when(has_far > 0)
-            def _():
-                pl.semaphore_wait(told_sem, 1)
-
-            send_far(part(*groups[0], me), 0)
+            rows = held[0].shape[1]
+            if rows > LANES:
+                send_near(part(0, rows - LANES, LANES, me), 0)
+            if early:
+                send_far(part(0, early, rows - early, me), 0)
+            else:
+                open_far(rows)
         else:
             send_both(part(*groups[array], me), array)
 
-    for load in loads[:3]:
-        load.wait()
-    for load in loads[3:]:
-        load.start()
-    half = held[0].shape[0] // 2
-    halves = [(0, half), (half, half)] if half % LANES == 0 else [(0, 2 * half)]
-    for columns in halves:
-        compute(0, 0, columns)
+    for one in opening:
+        one.wait()
+    compute(0, 0)
 
     pl.semaphore_wait(barrier, 1 + has_near)
 
@@ -210,8 +218,7 @@
     def _():
         pl.semaphore_signal(told_sem, inc=1, device_id=near, device_id_type=MESH)
 
-    for columns in halves[:-1]:
-        send_near(part(0, 0, LANES, me, columns), 0)
+    send_near(part(0, 0, LANES, me), 0)
 
     def exchange(side):
         return pltpu.make_async_remote_copy(
@@ -223,20 +230,23 @@
             device_id_type=MESH,
         )
 
+    early = (EARLY_PIECES - 1) * LANES if width > EARLY_PIECES * LANES else 0
+
     for array in range(len(outs)):
-        for load in loads[3 * array : 3 * array + 3] if array else others:
-            load.wait()
+        for one in rest_of[array]:
+            one.wait()
         count = held[array].shape[1] // LANES
         if array:
             compute(array, 0)
             finish(array - 1)
         if array == 1:
-            for load in loads[12:]:
-                load.wait()
+            for one in norm_loads:
+                one.wait()
             norm_out[me, core] = copied[12][...] + copied[13][...]
+        begin = 1
         if array == 0 and count > 1:
             compute(0, 1)
-            send_near(part(0, 0, LANES, me, halves[-1]), 0)
+            begin = 2
 
         def step(c, carry, array=array):
             compute(array, c)
@@ -244,7 +254,11 @@
                 send_near(part(0, (c - 1) * LANES, LANES, me), 0)
             return carry
 
-        lax.fori_loop(1 if array else 2, count, step, 0)
+        if array == 0 and early:
+            lax.fori_loop(begin, EARLY_PIECES, step, 0)
+            open_far(early)
+            begin = EARLY_PIECES
+        lax.fori_loop(begin, count, step, 0)
     exchange(core).start()
     if tail >= LANES:
         finish(last)
@@ -327,7 +341,12 @@
 
 
 def store(n, cores, *refs):
-    gathered, norm_ref, outs, norm_out, flat, sem, mixed_sem = refs[:4], refs[4], refs[5:9], *refs[9:]
+    gathered, norm_ref, outs, norm_out, flat, rounded, sem, mixed_sem, norm_sem = (
+        refs[:4],
+        refs[4],
+        refs[5:9],
+        *refs[9:],
+    )
     me, core = lax.axis_index("shard"), lax.axis_index("width")
     copies = []
     for source, out in zip(gathered[:3], outs[:3]):
@@ -362,10 +381,13 @@
     for origin in range(n):
         for side in range(cores):
             flat[pl.ds((origin * cores + side) * rows, rows)] = norm_ref[origin, side]
-    norm_out[...] = flat[...].astype(norm_out.dtype)
+    rounded[...] = flat[...].astype(norm_out.dtype)
+    norm_copy = pltpu.make_async_copy(rounded, norm_out, norm_sem)
+    norm_copy.start()
     for copy in copies:
         copy.wait()
     each_last(lambda copy: copy.wait())
+    norm_copy.wait()
 
 
 def late(n, mixed, after, out, send_sem, recv_sem, told_sem):
@@ -533,7 +555,7 @@
         out_specs=[in_vmem] * 5,
         scratch_shapes=[pltpu.VMEM(array.shape, array.dtype) for array in given]
         + [
-            pltpu.SemaphoreType.DMA((15,)),
+            pltpu.SemaphoreType.DMA((15 + bases[0].shape[0] // LANES,)),
             pltpu.SemaphoreType.DMA((n, groups)),
             pltpu.SemaphoreType.DMA((groups,)),
             pltpu.SemaphoreType.DMA((n, groups)),
@@ -551,11 +573,13 @@
         out_shape=[jax.ShapeDtypeStruct(shape, jnp.bfloat16) for shape in shapes]
         + [jax.ShapeDtypeStruct((norm_rows, LANES), jnp.bfloat16)],
         in_specs=[in_vmem] * 5,
-        out_specs=[in_hbm] * 4 + [in_vmem],
+        out_specs=[in_hbm] * 5,
         scratch_shapes=[
             pltpu.VMEM((norm_rows, LANES), jnp.float32),
+            pltpu.VMEM((norm_rows, LANES), jnp.bfloat16),
             pltpu.SemaphoreType.DMA((sum(-(-shape[0] // COPY_ROWS) for shape in shapes[:3]),)),
             pltpu.SemaphoreType.DMA((n, 2)),
+            pltpu.SemaphoreType.DMA,
         ],
         compiler_params=pltpu.CompilerParams(vmem_limit_bytes=20 * 2**20),
         name="store",

time: 175 us -> 175 us (level)
  no operation moved by 1% of the time
where the time goes in v2:
time: 175 us; the launch traced here: 174 us
  Pallas kernels  173 us (99%)
    pallas_call x1, Pallas kernels, on_device(): pl.pallas_call(functools.partial(body, n), out_shape=[pltpu.VMEM(shape, j...  169 us
    pallas_call x1, Pallas kernels, on_device(): pl.pallas_call(functools.partial(store, n, cores), out_shape=[jax.ShapeDt...  4.05 us

profile of v2, /device:TPU:0, one launch (start us, length us, event | category | flops | bytes accessed | tf_op | source)
XLA Modules:
  0.0 174.1 jit_solution(17354155745062590109)
XLA Ops:
  0.6 169.1 %merge_gather.1 = (bf16[1024,2048]{1,0:T(8,128)(2,1)S(1)}, bf16[256,2048]{1,0:T(8,128)(2,1)S(1)}, bf16[256,2048]{1,0:T(8,128)(2,1)S(1)}, bf16[2048,1024]{1,0:T(8,128)(2,1)S(1)}, f32[4,2,2,128]{3,2,1,0:T(2,128)S(1)}) custom-call(bf16[512,1024]{1,0:T(8,128)(2,1)} %refs_0_.1, bf16[16,512]{1,0:T(8,128)(2,1)} %bitcast.8, bf16[16,1024]{1,0:T(8,128)(2,1)} %refs_2_.1, ...), custom_call_target="tpu_custom_call" | custom-call | tf_op jit(solution)/shard_map/merge_gather/pallas_call | solution.py:550
  169.7 4.1 %store.1 = (bf16[1024,2048]{1,0:T(8,128)(2,1)}, bf16[256,2048]{1,0:T(8,128)(2,1)}, bf16[256,2048]{1,0:T(8,128)(2,1)}, bf16[2048,1024]{1,0:T(8,128)(2,1)}, bf16[16,128]{1,0:T(8,128)(2,1)}) custom-call(bf16[1024,2048]{1,0:T(8,128)(2,1)S(1)} %get-tuple-element.15.refs_0_, bf16[256,2048]{1,0:T(8,128)(2,1)S(1)} %get-tuple-element.16.refs_1_, ...), custom_call_target="tpu_custom_call" | custom-call | tf_op jit(solution)/shard_map/store/pallas_call | solution.py:571
  173.8 0.2 late.1.pieces
  174.0 0.1 store_late.1

commit v3 on v2

--- a/solution.py
+++ b/solution.py
@@ -11,12 +11,12 @@
 MESH = pl.DeviceIdType.MESH
 LANES = 128
 COPY_ROWS = 256
-LATE_STEPS = 3
+LATE_STEPS = 2
 LATE_CORE = 1
-LATE_ROWS = 192
+LATE_ROWS = 128
 ROW_UNIT = 64
-EARLY_PIECES = 4
-STORE_ROWS = 32
+EARLY_PIECES = 3
+STORE_ROWS = 64
 
 
 def plain(
@@ -71,12 +71,6 @@
     has_left, has_right = me > 0, me < n - 1
     left, right = {"shard": me - 1}, {"shard": me + 1}
     partner = {"width": 1 - core}
-    leftward = core == LATE_CORE
-    has_near = jnp.where(leftward, has_left.astype(jnp.int32), has_right.astype(jnp.int32))
-    has_far = jnp.where(leftward, has_right.astype(jnp.int32), has_left.astype(jnp.int32))
-    near = {"shard": jnp.where(leftward, me - 1, me + 1)}
-    far = {"shard": jnp.where(leftward, me + 1, me - 1)}
-
     held, low_refs, high_refs = copied[0:12:3], copied[1:12:3], copied[2:12:3]
     depth, width = held[0].shape
     first, rest = pl.ds(0, LANES), pl.ds(LANES, width - LANES)
@@ -102,12 +96,17 @@
     barrier = pltpu.get_barrier_semaphore()
     pl.semaphore_signal(barrier, inc=1, device_id=partner, device_id_type=MESH)
 
-    @pl.when(has_far > 0)
+    @pl.when(has_right)
     def _():
-        pl.semaphore_signal(barrier, inc=1, device_id=far, device_id_type=MESH)
+        pl.semaphore_signal(barrier, inc=1, device_id=right, device_id_type=MESH)
 
     for one in loads[len(opening) :]:
         one.start()
+    pl.semaphore_wait(barrier, 1 + has_left.astype(jnp.int32))
+
+    @pl.when(has_left)
+    def _():
+        pl.semaphore_signal(told_sem, inc=1, device_id=left, device_id_type=MESH)
 
     last = len(outs) - 1
     block = held[last].shape[1]
@@ -162,49 +161,36 @@
             jnp.bfloat16
         )
 
-    def send_near(ref, group):
-        @pl.when(jnp.logical_and(leftward, has_left))
+    def send_left(ref, group):
+        @pl.when(has_left)
         def _():
             copy(ref, left, back_sem.at[group], me, group).start()
 
-        @pl.when(jnp.logical_and(jnp.logical_not(leftward), has_right))
+    def send_right(ref, group):
+        @pl.when(has_right)
         def _():
             copy(ref, right, send_sem.at[me, group], me, group).start()
 
-    def send_far(ref, group):
-        @pl.when(jnp.logical_and(jnp.logical_not(leftward), has_left))
-        def _():
-            copy(ref, left, back_sem.at[group], me, group).start()
-
-        @pl.when(jnp.logical_and(leftward, has_right))
-        def _():
-            copy(ref, right, send_sem.at[me, group], me, group).start()
-
     def send_both(ref, group):
-        @pl.when(has_left)
-        def _():
-            copy(ref, left, back_sem.at[group], me, group).start()
-
+        send_left(ref, group)
+        send_right(ref, group)
+
+    def open_right(rows):
         @pl.when(has_right)
         def _():
-            copy(ref, right, send_sem.at[me, group], me, group).start()
-
-    def open_far(rows):
-        @pl.when(has_far > 0)
-        def _():
             pl.semaphore_wait(told_sem, 1)
 
-        send_far(part(0, 0, rows, me), 0)
+        send_right(part(0, 0, rows, me), 0)
 
     def finish(array):
         if array == 0:
             rows = held[0].shape[1]
             if rows > LANES:
-                send_near(part(0, rows - LANES, LANES, me), 0)
+                send_left(part(0, rows - LANES, LANES, me), 0)
             if early:
-                send_far(part(0, early, rows - early, me), 0)
+                send_right(part(0, early, rows - early, me), 0)
             else:
-                open_far(rows)
+                open_right(rows)
         else:
             send_both(part(*groups[array], me), array)
 
@@ -212,13 +198,7 @@
         one.wait()
     compute(0, 0)
 
-    pl.semaphore_wait(barrier, 1 + has_near)
-
-    @pl.when(has_near > 0)
-    def _():
-        pl.semaphore_signal(told_sem, inc=1, device_id=near, device_id_type=MESH)
-
-    send_near(part(0, 0, LANES, me), 0)
+    send_left(part(0, 0, LANES, me), 0)
 
     def exchange(side):
         return pltpu.make_async_remote_copy(
@@ -251,12 +231,12 @@
         def step(c, carry, array=array):
             compute(array, c)
             if array == 0:
-                send_near(part(0, (c - 1) * LANES, LANES, me), 0)
+                send_left(part(0, (c - 1) * LANES, LANES, me), 0)
             return carry
 
         if array == 0 and early:
             lax.fori_loop(begin, EARLY_PIECES, step, 0)
-            open_far(early)
+            open_right(early)
             begin = EARLY_PIECES
         lax.fori_loop(begin, count, step, 0)
     exchange(core).start()
@@ -423,41 +403,23 @@
     @pl.when(core == LATE_CORE)
     def _():
         barrier = pltpu.get_barrier_semaphore()
-        half = n // 2
-        to_left, middle = me < half, me == half
-
-        def signal(semaphore, condition, device):
-            @pl.when(condition)
-            def _():
-                pl.semaphore_signal(semaphore, inc=1, device_id=device, device_id_type=MESH)
-
-        signal(barrier, jnp.logical_and(has_right, me < half), right)
-        signal(barrier, me > half, left)
-        known = jnp.where(to_left, has_left, has_right).astype(jnp.int32)
-        known += jnp.logical_and(middle, has_left).astype(jnp.int32)
-
-        @pl.when(known > 0)
-        def _():
-            pl.semaphore_wait(barrier, known)
-
-        def own(direction, condition):
+
+        @pl.when(has_right)
+        def _():
+            pl.semaphore_signal(barrier, inc=1, device_id=right, device_id_type=MESH)
+
+        @pl.when(has_left)
+        def _():
+            pl.semaphore_wait(barrier, 1)
             for step in range(LATE_STEPS):
-
-                @pl.when(condition)
-                def _(step=step):
-                    direction(me, step, own=True).start()
-
-        own(backward, jnp.logical_and(to_left, has_left))
-        own(forward, jnp.logical_and(jnp.logical_not(to_left), has_right))
-        signal(told_sem, jnp.logical_and(has_left, me <= half), left)
-        signal(told_sem, jnp.logical_and(has_right, me >= half), right)
-        unknown = jnp.logical_or(jnp.logical_and(to_left, has_right), me > half)
-
-        @pl.when(unknown)
+                backward(me, step, own=True).start()
+            pl.semaphore_signal(told_sem, inc=1, device_id=left, device_id_type=MESH)
+
+        @pl.when(has_right)
         def _():
             pl.semaphore_wait(told_sem, 1)
-        own(backward, jnp.logical_and(jnp.logical_not(to_left), has_left))
-        own(forward, jnp.logical_and(to_left, has_right))
+            for step in range(LATE_STEPS):
+                forward(me, step, own=True).start()
 
         def relay(k, carry):
             for step in range(LATE_STEPS):

time: 175 us -> 175 us (level)
  no operation moved by 1% of the time
where the time goes in v3:
time: 175 us; the launch traced here: 173 us
  Pallas kernels  172 us (98%)
    pallas_call x1, Pallas kernels, on_device(): pl.pallas_call(functools.partial(body, n), out_shape=[pltpu.VMEM(shape, j...  168 us
    pallas_call x1, Pallas kernels, on_device(): pl.pallas_call(functools.partial(store, n, cores), out_shape=[jax.ShapeDt...  4.04 us

profile of v3, /device:TPU:0, one launch (start us, length us, event | category | flops | bytes accessed | tf_op | source)
XLA Modules:
  0.0 172.6 jit_solution(11558006352876786394)
XLA Ops:
  0.6 167.7 %merge_gather.1 = (bf16[1024,2048]{1,0:T(8,128)(2,1)S(1)}, bf16[256,2048]{1,0:T(8,128)(2,1)S(1)}, bf16[256,2048]{1,0:T(8,128)(2,1)S(1)}, bf16[2048,1024]{1,0:T(8,128)(2,1)S(1)}, f32[4,2,2,128]{3,2,1,0:T(2,128)S(1)}) custom-call(bf16[512,1024]{1,0:T(8,128)(2,1)} %refs_0_.1, bf16[16,512]{1,0:T(8,128)(2,1)} %bitcast.8, bf16[16,1024]{1,0:T(8,128)(2,1)} %refs_2_.1, ...), custom_call_target="tpu_custom_call" | custom-call | tf_op jit(solution)/shard_map/merge_gather/pallas_call | solution.py:512
  168.4 4.0 %store.1 = (bf16[1024,2048]{1,0:T(8,128)(2,1)}, bf16[256,2048]{1,0:T(8,128)(2,1)}, bf16[256,2048]{1,0:T(8,128)(2,1)}, bf16[2048,1024]{1,0:T(8,128)(2,1)}, bf16[16,128]{1,0:T(8,128)(2,1)}) custom-call(bf16[1024,2048]{1,0:T(8,128)(2,1)S(1)} %get-tuple-element.15.refs_0_, bf16[256,2048]{1,0:T(8,128)(2,1)S(1)} %get-tuple-element.16.refs_1_, ...), custom_call_target="tpu_custom_call" | custom-call | tf_op jit(solution)/shard_map/store/pallas_call | solution.py:533
  172.4 0.2 late.1.pieces
  172.6 0.1 store_late.1

commit v4 on v3

--- a/solution.py
+++ b/solution.py
@@ -14,7 +14,9 @@
 LATE_STEPS = 2
 LATE_CORE = 1
 LATE_ROWS = 128
-ROW_UNIT = 64
+ROW_UNIT = 16
+DETOURS = 2
+DETOUR_ROWS = 16
 EARLY_PIECES = 3
 STORE_ROWS = 64
 
@@ -49,12 +51,17 @@
     return query.T, key.T, value.T, mixed.T, norm
 
 
+def detours(shifts):
+    return min(DETOURS, shifts - 1)
+
+
 def late_rows(block):
     return LATE_ROWS if block > LATE_ROWS else 0
 
 
 def kernel(
     n,
+    shifts,
     given,
     outs,
     norm_out,
@@ -65,12 +72,24 @@
     recv_sem,
     pair_sem,
     told_sem,
+    detour,
+    detour_send,
+    detour_recv,
 ):
-    me = lax.axis_index("shard")
+    me, shift = lax.axis_index("shard"), lax.axis_index("shift")
     core = lax.axis_index("width")
     has_left, has_right = me > 0, me < n - 1
     left, right = {"shard": me - 1}, {"shard": me + 1}
     partner = {"width": 1 - core}
+    helpers = range(1, 1 + detours(shifts))
+    aside = len(helpers) * DETOUR_ROWS
+
+    def on_early(*conditions):
+        return functools.reduce(jnp.logical_and, conditions, core != LATE_CORE)
+
+    helps = jnp.logical_and(shift >= 1, shift <= len(helpers))
+    leads, ends = on_early(shift == 0, me == 1), on_early(shift == 0, me == 0)
+    lifts, lands = on_early(helps, me == 1), on_early(helps, me == 0)
     held, low_refs, high_refs = copied[0:12:3], copied[1:12:3], copied[2:12:3]
     depth, width = held[0].shape
     first, rest = pl.ds(0, LANES), pl.ds(LANES, width - LANES)
@@ -100,9 +119,25 @@
     def _():
         pl.semaphore_signal(barrier, inc=1, device_id=right, device_id_type=MESH)
 
+    if aside:
+
+        @pl.when(lifts)
+        def _():
+            line = {"shift": 0 * shift}
+            pl.semaphore_signal(barrier, inc=1, device_id=line, device_id_type=MESH)
+
+        @pl.when(ends)
+        def _():
+            for helper in helpers:
+                line = {"shift": 0 * shift + helper}
+                pl.semaphore_signal(barrier, inc=1, device_id=line, device_id_type=MESH)
+
     for one in loads[len(opening) :]:
         one.start()
-    pl.semaphore_wait(barrier, 1 + has_left.astype(jnp.int32))
+    waited = 1 + has_left.astype(jnp.int32)
+    if aside:
+        waited += jnp.where(leads, len(helpers), 0) + lands.astype(jnp.int32)
+    pl.semaphore_wait(barrier, waited)
 
     @pl.when(has_left)
     def _():
@@ -112,11 +147,15 @@
     block = held[last].shape[1]
     tail = late_rows(block)
     groups = [(array, 0, w.shape[1]) for array, w in enumerate(held[:last])]
-    groups.append((last, 0, block - tail))
+    groups.append((last, aside, block - tail - aside))
     if tail:
         groups.append((last, block - tail, tail))
     groups.append((len(outs), 0, 0))
-    late_group = len(groups) - 2 if tail else -1
+    side_group = len(groups)
+    if aside:
+        groups.append((last, 0, aside))
+    norm_group = len(outs) + (1 if tail else 0)
+    late_group = norm_group - 1 if tail else -1
 
     def part(array, row, rows, origin):
         if array == len(outs):
@@ -174,6 +213,46 @@
     def send_both(ref, group):
         send_left(ref, group)
         send_right(ref, group)
+
+    def hop(source, target, device, index, semaphore):
+        return pltpu.make_async_remote_copy(
+            src_ref=source,
+            dst_ref=target,
+            send_sem=detour_send.at[index],
+            recv_sem=semaphore,
+            device_id=device,
+            device_id_type=MESH,
+        )
+
+    def lead(helper):
+        source = part(last, (helper - 1) * DETOUR_ROWS, DETOUR_ROWS, me)
+        line = {"shift": 0 * shift + helper}
+        return hop(source, detour, line, helper - 1, detour_recv.at[0])
+
+    def lift():
+        return hop(detour, detour, left, 0, detour_recv.at[0])
+
+    def land():
+        target = part(last, (shift - 1) * DETOUR_ROWS, DETOUR_ROWS, me + 1)
+        return hop(detour, target, {"shift": 0 * shift}, 0, recv_sem.at[1, side_group])
+
+    def send_aside():
+        ref = part(*groups[side_group], me)
+        send_right(ref, side_group)
+
+        @pl.when(jnp.logical_not(leads))
+        def _():
+            send_left(ref, side_group)
+
+        @pl.when(leads)
+        def _():
+            for helper in helpers:
+                lead(helper).start()
+
+        @pl.when(lifts)
+        def _():
+            lift().wait_recv()
+            lift().start()
 
     def open_right(rows):
         @pl.when(has_right)
@@ -252,7 +331,9 @@
         def _():
             send_both(part(*groups[late_group], me), late_group)
 
-    send_both(part(*groups[-1], me), len(groups) - 1)
+    send_both(part(*groups[norm_group], me), norm_group)
+    if aside:
+        send_aside()
 
     def each_group(act):
         for group in range(len(groups)):
@@ -285,6 +366,13 @@
                     backward(group, from_right).start()
 
         each_group(pass_on)
+        if aside:
+
+            @pl.when(jnp.logical_and(lands, k == 1))
+            def _():
+                lift().wait_recv()
+                land().start()
+
         return carry
 
     lax.fori_loop(1, n, relay, 0)
@@ -294,11 +382,29 @@
         def _():
             forward(group, me).wait_send()
 
-        @pl.when(has_left)
+        goes_left = has_left
+        if group == side_group:
+            goes_left = jnp.logical_and(has_left, jnp.logical_not(leads))
+
+        @pl.when(goes_left)
         def _():
             backward(group, me, own=True).wait_send()
 
     each_group(own_sent)
+    if aside:
+
+        @pl.when(leads)
+        def _():
+            for helper in helpers:
+                lead(helper).wait_send()
+
+        @pl.when(lifts)
+        def _():
+            lift().wait_send()
+
+        @pl.when(jnp.logical_and(lands, n > 1))
+        def _():
+            land().wait_send()
 
     def drain(k, carry):
         def sent(group):
@@ -316,8 +422,8 @@
     lax.fori_loop(1, n, drain, 0)
 
 
-def body(n, *refs):
-    kernel(n, refs[:14], refs[14:18], refs[18], refs[19:33], *refs[33:])
+def body(n, shifts, *refs):
+    kernel(n, shifts, refs[:14], refs[14:18], refs[18], refs[19:33], *refs[33:])
 
 
 def store(n, cores, *refs):
@@ -492,7 +598,7 @@
     each(end)
 
 
-def on_device(n, cores, *args):
+def on_device(n, cores, shifts, *args):
     weights, (norm_train, norm_step) = list(args[:12]), args[12:]
     bases = weights[0::3]
     (size,) = norm_train.shape
@@ -505,12 +611,13 @@
     in_hbm = pl.BlockSpec(memory_space=pltpu.HBM)
     in_vmem = pl.BlockSpec(memory_space=pltpu.VMEM)
     tail = late_rows(bases[3].shape[1])
-    groups = len(bases) + (2 if tail else 1)
+    helpers = detours(shifts)
+    groups = len(bases) + (2 if tail else 1) + (1 if helpers else 0)
     weights[1::3] = [low.T for low in weights[1::3]]
     norms = [norm_train.reshape(rows, LANES), norm_step.reshape(rows, LANES)]
     given = [pltpu.with_memory_space_constraint(array, pltpu.HBM) for array in weights + norms]
     gathered = pl.pallas_call(
-        functools.partial(body, n),
+        functools.partial(body, n, shifts),
         out_shape=[pltpu.VMEM(shape, jnp.bfloat16) for shape in shapes]
         + [pltpu.VMEM((n, cores, rows, LANES), jnp.float32)],
         in_specs=[in_hbm] * 14,
@@ -523,6 +630,9 @@
             pltpu.SemaphoreType.DMA((n, groups)),
             pltpu.SemaphoreType.DMA((2,)),
             pltpu.SemaphoreType.REGULAR,
+            pltpu.VMEM((DETOUR_ROWS, shapes[3][1]), jnp.bfloat16),
+            pltpu.SemaphoreType.DMA((max(helpers, 1),)),
+            pltpu.SemaphoreType.DMA((1,)),
         ],
         compiler_params=pltpu.CompilerParams(
             collective_id=0, has_side_effects=True, vmem_limit_bytes=40 * 2**20
@@ -596,7 +706,9 @@
         P(("shift", "shard", "width")),
     )
     return jax.shard_map(
-        functools.partial(on_device, mesh.shape["shard"], mesh.shape["width"]),
+        functools.partial(
+            on_device, mesh.shape["shard"], mesh.shape["width"], mesh.shape["shift"]
+        ),
         mesh=mesh,
         in_specs=placed,
         out_specs=(

time: 175 us -> 174 us (level)
  no operation moved by 1% of the time
where the time goes in v4:
time: 174 us; the launch traced here: 172 us
  Pallas kernels  171 us (98%)
    pallas_call x1, Pallas kernels, on_device(): pl.pallas_call(functools.partial(body, n, shifts), out_shape=[pltpu.VMEM(...  167 us
    pallas_call x1, Pallas kernels, on_device(): pl.pallas_call(functools.partial(store, n, cores), out_shape=[jax.ShapeDt...  4.04 us

profile of v4, /device:TPU:0, one launch (start us, length us, event | category | flops | bytes accessed | tf_op | source)
XLA Modules:
  0.0 172.0 jit_solution(5516091856209520150)
XLA Ops:
  0.6 167.1 %merge_gather.1 = (bf16[1024,2048]{1,0:T(8,128)(2,1)S(1)}, bf16[256,2048]{1,0:T(8,128)(2,1)S(1)}, bf16[256,2048]{1,0:T(8,128)(2,1)S(1)}, bf16[2048,1024]{1,0:T(8,128)(2,1)S(1)}, f32[4,2,2,128]{3,2,1,0:T(2,128)S(1)}) custom-call(bf16[512,1024]{1,0:T(8,128)(2,1)} %refs_0_.1, bf16[16,512]{1,0:T(8,128)(2,1)} %bitcast.8, bf16[16,1024]{1,0:T(8,128)(2,1)} %refs_2_.1, ...), custom_call_target="tpu_custom_call" | custom-call | tf_op jit(solution)/shard_map/merge_gather/pallas_call | solution.py:619
  167.7 4.0 %store.1 = (bf16[1024,2048]{1,0:T(8,128)(2,1)}, bf16[256,2048]{1,0:T(8,128)(2,1)}, bf16[256,2048]{1,0:T(8,128)(2,1)}, bf16[2048,1024]{1,0:T(8,128)(2,1)}, bf16[16,128]{1,0:T(8,128)(2,1)}) custom-call(bf16[1024,2048]{1,0:T(8,128)(2,1)S(1)} %get-tuple-element.15.refs_0_, bf16[256,2048]{1,0:T(8,128)(2,1)S(1)} %get-tuple-element.16.refs_1_, ...), custom_call_target="tpu_custom_call" | custom-call | tf_op jit(solution)/shard_map/store/pallas_call | solution.py:643
  171.7 0.2 late.1.pieces
  171.9 0.1 store_late.1

commit v5 on v4

--- a/solution.py
+++ b/solution.py
@@ -55,6 +55,11 @@
     return min(DETOURS, shifts - 1)
 
 
+def short_rows(depth):
+    rows = LANES * LANES // depth
+    return rows if rows * depth == LANES * LANES and rows % ROW_UNIT == 0 and rows < LANES else 0
+
+
 def late_rows(block):
     return LATE_ROWS if block > LATE_ROWS else 0
 
@@ -75,6 +80,10 @@
     detour,
     detour_send,
     detour_recv,
+    raw,
+    raw_low,
+    raw_send,
+    raw_recv,
 ):
     me, shift = lax.axis_index("shard"), lax.axis_index("shift")
     core = lax.axis_index("width")
@@ -157,13 +166,13 @@
     norm_group = len(outs) + (1 if tail else 0)
     late_group = norm_group - 1 if tail else -1
 
-    def part(array, row, rows, origin):
+    def part(array, row, rows, origin, band=None):
         if array == len(outs):
             return norm_out.at[origin]
         out, w = outs[array], held[array]
         if array < last:
-            size = w.shape[0]
-            begin = pl.multiple_of(origin * size, LANES)
+            first, size = band or (0, w.shape[0])
+            begin = pl.multiple_of(origin * w.shape[0] + first, LANES)
             return out.at[pl.ds(pl.multiple_of(row, LANES), rows), pl.ds(begin, size)]
         begin = pl.multiple_of(origin * block + row, ROW_UNIT)
         return out.at[pl.ds(begin, rows)]
@@ -177,6 +186,27 @@
             device_id=device,
             device_id_type=MESH,
         )
+
+    short = short_rows(depth)
+    corner = pl.ds(0, LANES)
+
+    def raw_copies():
+        pairs = ((held[0].at[corner, corner], raw), (low_refs[0].at[:, corner], raw_low))
+        return [
+            pltpu.make_async_remote_copy(
+                src_ref=source,
+                dst_ref=target,
+                send_sem=raw_send.at[i],
+                recv_sem=raw_recv.at[i],
+                device_id=left,
+                device_id_type=MESH,
+            )
+            for i, (source, target) in enumerate(pairs)
+        ]
+
+    def near_query():
+        ref = part(0, 0, width - short, me)
+        return copy(ref, left, back_sem.at[0], me + 1, 0)
 
     def forward(group, origin):
         ref = part(*groups[group], origin)
@@ -273,11 +303,19 @@
         else:
             send_both(part(*groups[array], me), array)
 
-    for one in opening:
+    opening[0].wait()
+    opening[2].wait()
+    if short:
+
+        @pl.when(has_left)
+        def _():
+            for one in raw_copies():
+                one.start()
+
+    for one in opening[1:2] + opening[3:]:
         one.wait()
     compute(0, 0)
-
-    send_left(part(0, 0, LANES, me), 0)
+    send_left(part(0, 0, LANES, me, (LANES, depth - LANES) if short else None), 0)
 
     def exchange(side):
         return pltpu.make_async_remote_copy(
@@ -335,6 +373,23 @@
     if aside:
         send_aside()
 
+    if short:
+
+        @pl.when(has_right)
+        def _():
+            for one in raw_copies():
+                one.wait_recv()
+            low_rank = lax.dot_general(
+                high_refs[0][:, corner],
+                raw_low[...],
+                (((0,), (0,)), ((), ())),
+                preferred_element_type=jnp.float32,
+            )
+            base = raw[...].T.astype(jnp.float32)
+            part(0, 0, LANES, me + 1, (0, LANES))[...] = (base + mix_rate * low_rank).astype(
+                jnp.bfloat16
+            )
+
     def each_group(act):
         for group in range(len(groups)):
             if group == late_group:
@@ -359,7 +414,17 @@
 
             @pl.when(from_right < n)
             def _():
-                backward(group, from_right).wait_recv()
+                if group == 0 and short:
+
+                    @pl.when(k == 1)
+                    def _():
+                        near_query().wait_recv()
+
+                    @pl.when(k > 1)
+                    def _():
+                        backward(group, from_right).wait_recv()
+                else:
+                    backward(group, from_right).wait_recv()
 
                 @pl.when(has_left)
                 def _():
@@ -388,9 +453,18 @@
 
         @pl.when(goes_left)
         def _():
-            backward(group, me, own=True).wait_send()
+            if group == 0 and short:
+                near_query().wait_send()
+            else:
+                backward(group, me, own=True).wait_send()
 
     each_group(own_sent)
+    if short:
+
+        @pl.when(has_left)
+        def _():
+            for one in raw_copies():
+                one.wait_send()
     if aside:
 
         @pl.when(leads)
@@ -633,6 +707,10 @@
             pltpu.VMEM((DETOUR_ROWS, shapes[3][1]), jnp.bfloat16),
             pltpu.SemaphoreType.DMA((max(helpers, 1),)),
             pltpu.SemaphoreType.DMA((1,)),
+            pltpu.VMEM((LANES, LANES), jnp.bfloat16),
+            pltpu.VMEM((given[1].shape[0], LANES), jnp.bfloat16),
+            pltpu.SemaphoreType.DMA((2,)),
+            pltpu.SemaphoreType.DMA((2,)),
         ],
         compiler_params=pltpu.CompilerParams(
             collective_id=0, has_side_effects=True, vmem_limit_bytes=40 * 2**20

time: 174 us -> 174 us (level)
  no operation moved by 1% of the time
where the time goes in v5:
time: 174 us; the launch traced here: 172 us
  Pallas kernels  171 us (98%)
    pallas_call x1, Pallas kernels, on_device(): pl.pallas_call(functools.partial(body, n, shifts), out_shape=[pltpu.VMEM(...  167 us
    pallas_call x1, Pallas kernels, on_device(): pl.pallas_call(functools.partial(store, n, cores), out_shape=[jax.ShapeDt...  4.04 us

profile of v5, /device:TPU:0, one launch (start us, length us, event | category | flops | bytes accessed | tf_op | source)
XLA Modules:
  0.0 171.8 jit_solution(16627764215763646298)
XLA Ops:
  0.6 166.9 %merge_gather.1 = (bf16[1024,2048]{1,0:T(8,128)(2,1)S(1)}, bf16[256,2048]{1,0:T(8,128)(2,1)S(1)}, bf16[256,2048]{1,0:T(8,128)(2,1)S(1)}, bf16[2048,1024]{1,0:T(8,128)(2,1)S(1)}, f32[4,2,2,128]{3,2,1,0:T(2,128)S(1)}) custom-call(bf16[512,1024]{1,0:T(8,128)(2,1)} %refs_0_.1, bf16[16,512]{1,0:T(8,128)(2,1)} %bitcast.8, bf16[16,1024]{1,0:T(8,128)(2,1)} %refs_2_.1, ...), custom_call_target="tpu_custom_call" | custom-call | tf_op jit(solution)/shard_map/merge_gather/pallas_call | solution.py:693
  167.6 4.0 %store.1 = (bf16[1024,2048]{1,0:T(8,128)(2,1)}, bf16[256,2048]{1,0:T(8,128)(2,1)}, bf16[256,2048]{1,0:T(8,128)(2,1)}, bf16[2048,1024]{1,0:T(8,128)(2,1)}, bf16[16,128]{1,0:T(8,128)(2,1)}) custom-call(bf16[1024,2048]{1,0:T(8,128)(2,1)S(1)} %get-tuple-element.15.refs_0_, bf16[256,2048]{1,0:T(8,128)(2,1)S(1)} %get-tuple-element.16.refs_1_, ...), custom_call_target="tpu_custom_call" | custom-call | tf_op jit(solution)/shard_map/store/pallas_call | solution.py:721
  171.6 0.2 late.1.pieces
  171.8 0.1 store_late.1

commit v6 on v5

--- a/solution.py
+++ b/solution.py
@@ -13,12 +13,12 @@
 COPY_ROWS = 256
 LATE_STEPS = 2
 LATE_CORE = 1
-LATE_ROWS = 128
+LATE_ROWS = 160
 ROW_UNIT = 16
 DETOURS = 2
 DETOUR_ROWS = 16
 EARLY_PIECES = 3
-STORE_ROWS = 64
+STORE_ROWS = 32
 
 
 def plain(

time: 174 us -> 174 us (level)
  no operation moved by 1% of the time
where the time goes in v6:
time: 174 us; the launch traced here: 172 us
  Pallas kernels  171 us (98%)
    pallas_call x1, Pallas kernels, on_device(): pl.pallas_call(functools.partial(body, n, shifts), out_shape=[pltpu.VMEM(...  167 us
    pallas_call x1, Pallas kernels, on_device(): pl.pallas_call(functools.partial(store, n, cores), out_shape=[jax.ShapeDt...  4.04 us

profile of v6, /device:TPU:0, one launch (start us, length us, event | category | flops | bytes accessed | tf_op | source)
XLA Modules:
  0.0 171.9 jit_solution(13524567131467420010)
XLA Ops:
  0.6 167.0 %merge_gather.1 = (bf16[1024,2048]{1,0:T(8,128)(2,1)S(1)}, bf16[256,2048]{1,0:T(8,128)(2,1)S(1)}, bf16[256,2048]{1,0:T(8,128)(2,1)S(1)}, bf16[2048,1024]{1,0:T(8,128)(2,1)S(1)}, f32[4,2,2,128]{3,2,1,0:T(2,128)S(1)}) custom-call(bf16[512,1024]{1,0:T(8,128)(2,1)} %refs_0_.1, bf16[16,512]{1,0:T(8,128)(2,1)} %bitcast.8, bf16[16,1024]{1,0:T(8,128)(2,1)} %refs_2_.1, ...), custom_call_target="tpu_custom_call" | custom-call | tf_op jit(solution)/shard_map/merge_gather/pallas_call | solution.py:693
  167.6 4.0 %store.1 = (bf16[1024,2048]{1,0:T(8,128)(2,1)}, bf16[256,2048]{1,0:T(8,128)(2,1)}, bf16[256,2048]{1,0:T(8,128)(2,1)}, bf16[2048,1024]{1,0:T(8,128)(2,1)}, bf16[16,128]{1,0:T(8,128)(2,1)}) custom-call(bf16[1024,2048]{1,0:T(8,128)(2,1)S(1)} %get-tuple-element.15.refs_0_, bf16[256,2048]{1,0:T(8,128)(2,1)S(1)} %get-tuple-element.16.refs_1_, ...), custom_call_target="tpu_custom_call" | custom-call | tf_op jit(solution)/shard_map/store/pallas_call | solution.py:721
  171.7 0.2 late.1.pieces
  171.8 0.1 store_late.1

commit v7 on v6

--- a/solution.py
+++ b/solution.py
@@ -14,9 +14,9 @@
 LATE_STEPS = 2
 LATE_CORE = 1
 LATE_ROWS = 160
-ROW_UNIT = 16
-DETOURS = 2
-DETOUR_ROWS = 16
+ROW_UNIT = 8
+DETOURS = 3
+DETOUR_ROWS = 8
 EARLY_PIECES = 3
 STORE_ROWS = 32
 

time: 174 us -> 174 us (level)
  Pallas kernels: 171 us -> 173 us
where the time goes in v7:
time: 174 us; the launch traced here: 173 us
  Pallas kernels  173 us (99%)
    pallas_call x1, Pallas kernels, on_device(): pl.pallas_call(functools.partial(body, n, shifts), out_shape=[pltpu.VMEM(...  168 us
    pallas_call x1, Pallas kernels, on_device(): pl.pallas_call(functools.partial(store, n, cores), out_shape=[jax.ShapeDt...  4.04 us

profile of v7, /device:TPU:0, one launch (start us, length us, event | category | flops | bytes accessed | tf_op | source)
XLA Modules:
  0.0 173.2 jit_solution(11981155107870651554)
XLA Ops:
  0.6 168.3 %merge_gather.1 = (bf16[1024,2048]{1,0:T(8,128)(2,1)S(1)}, bf16[256,2048]{1,0:T(8,128)(2,1)S(1)}, bf16[256,2048]{1,0:T(8,128)(2,1)S(1)}, bf16[2048,1024]{1,0:T(8,128)(2,1)S(1)}, f32[4,2,2,128]{3,2,1,0:T(2,128)S(1)}) custom-call(bf16[512,1024]{1,0:T(8,128)(2,1)} %refs_0_.1, bf16[16,512]{1,0:T(8,128)(2,1)} %bitcast.8, bf16[16,1024]{1,0:T(8,128)(2,1)} %refs_2_.1, ...), custom_call_target="tpu_custom_call" | custom-call | tf_op jit(solution)/shard_map/merge_gather/pallas_call | solution.py:693
  168.9 4.0 %store.1 = (bf16[1024,2048]{1,0:T(8,128)(2,1)}, bf16[256,2048]{1,0:T(8,128)(2,1)}, bf16[256,2048]{1,0:T(8,128)(2,1)}, bf16[2048,1024]{1,0:T(8,128)(2,1)}, bf16[16,128]{1,0:T(8,128)(2,1)}) custom-call(bf16[1024,2048]{1,0:T(8,128)(2,1)S(1)} %get-tuple-element.15.refs_0_, bf16[256,2048]{1,0:T(8,128)(2,1)S(1)} %get-tuple-element.16.refs_1_, ...), custom_call_target="tpu_custom_call" | custom-call | tf_op jit(solution)/shard_map/store/pallas_call | solution.py:721
  173.0 0.2 late.1.pieces
  173.1 0.1 store_late.1

commit v8 on v7

--- a/solution.py
+++ b/solution.py
@@ -11,14 +11,14 @@
 MESH = pl.DeviceIdType.MESH
 LANES = 128
 COPY_ROWS = 256
-LATE_STEPS = 2
+LATE_STEPS = 3
 LATE_CORE = 1
-LATE_ROWS = 160
+LATE_ROWS = 144
 ROW_UNIT = 8
 DETOURS = 3
 DETOUR_ROWS = 8
 EARLY_PIECES = 3
-STORE_ROWS = 32
+STORE_ROWS = 48
 
 
 def plain(
@@ -118,7 +118,7 @@
         [load(given[i], copied[i]) for i in range(array, array + 3)] for array in (3, 6, 9)
     ]
     norm_loads = [load(given[i], copied[i]) for i in (12, 13)]
-    for one in opening:
+    for one in (opening[2], *opening[:2], *opening[3:]):
         one.start()
 
     barrier = pltpu.get_barrier_semaphore()

time: 174 us -> 174 us (level)
  no operation moved by 1% of the time
where the time goes in v8:
time: 174 us; the launch traced here: 173 us
  Pallas kernels  173 us (99%)
    pallas_call x1, Pallas kernels, on_device(): pl.pallas_call(functools.partial(body, n, shifts), out_shape=[pltpu.VMEM(...  168 us
    pallas_call x1, Pallas kernels, on_device(): pl.pallas_call(functools.partial(store, n, cores), out_shape=[jax.ShapeDt...  4.04 us

profile of v8, /device:TPU:0, one launch (start us, length us, event | category | flops | bytes accessed | tf_op | source)
XLA Modules:
  0.0 173.2 jit_solution(15670400823959401670)
XLA Ops:
  0.6 168.2 %merge_gather.1 = (bf16[1024,2048]{1,0:T(8,128)(2,1)S(1)}, bf16[256,2048]{1,0:T(8,128)(2,1)S(1)}, bf16[256,2048]{1,0:T(8,128)(2,1)S(1)}, bf16[2048,1024]{1,0:T(8,128)(2,1)S(1)}, f32[4,2,2,128]{3,2,1,0:T(2,128)S(1)}) custom-call(bf16[512,1024]{1,0:T(8,128)(2,1)} %refs_0_.1, bf16[16,512]{1,0:T(8,128)(2,1)} %bitcast.8, bf16[16,1024]{1,0:T(8,128)(2,1)} %refs_2_.1, ...), custom_call_target="tpu_custom_call" | custom-call | tf_op jit(solution)/shard_map/merge_gather/pallas_call | solution.py:693
  168.9 4.0 %store.1 = (bf16[1024,2048]{1,0:T(8,128)(2,1)}, bf16[256,2048]{1,0:T(8,128)(2,1)}, bf16[256,2048]{1,0:T(8,128)(2,1)}, bf16[2048,1024]{1,0:T(8,128)(2,1)}, bf16[16,128]{1,0:T(8,128)(2,1)}) custom-call(bf16[1024,2048]{1,0:T(8,128)(2,1)S(1)} %get-tuple-element.15.refs_0_, bf16[256,2048]{1,0:T(8,128)(2,1)S(1)} %get-tuple-element.16.refs_1_, ...), custom_call_target="tpu_custom_call" | custom-call | tf_op jit(solution)/shard_map/store/pallas_call | solution.py:721
  172.9 0.2 late.1.pieces
  173.1 0.1 store_late.1
